TPU v7x, 16 devices: a whole 2x2x2 slice. The times are simulated.
16 devices in a mesh: dp: 1, tp: 16 (over x, y, z, core).
Axes of the slice: x: 2, y: 2, z: 2, core: 2. Of those that a mesh axis runs over, the one named last changes fastest.
Arguments:
- x: bfloat16 [2048, 4096], P('dp')
- dy: bfloat16 [2048, 4096], P('dp')
- gate: bfloat16 [2048, 10240], P('dp', 'tp')
- up: bfloat16 [2048, 10240], P('dp', 'tp')
- w_gate: bfloat16 [4096, 10240], P(None, 'tp')
- w_up: bfloat16 [4096, 10240], P(None, 'tp')
- w_down: bfloat16 [10240, 4096], P('tp')
Outputs:
- output 1: bfloat16 [2048, 4096], P('dp')
- output 2: bfloat16 [4096, 10240], P('dp', 'tp')
- output 3: bfloat16 [4096, 10240], P('dp', 'tp')
- output 4: bfloat16 [10240, 4096], P(('dp', 'tp'))
All inputs are finite; a program needn't handle non-finite values.
Results may differ from a plain program's by a relative error of at most 0.012.
Values are sent between devices in bfloat16 or wider.
A program may use at most 2 GiB of HBM per device.

v0:
```python
import jax
import jax.numpy as jnp
from jax import lax
from jax.sharding import PartitionSpec as P


def act(gate, up):
    return jax.nn.gelu(gate) * up


def solution(mesh):
    def step(x, dy, gate, up, w_gate, w_up, w_down):
        hidden, back = jax.vjp(act, gate.astype(jnp.float32), up.astype(jnp.float32))
        d_hidden = jnp.dot(dy, w_down.T, preferred_element_type=jnp.float32)
        d_gate, d_up = (g.astype(jnp.bfloat16) for g in back(d_hidden))
        term = jnp.dot(d_gate, w_gate.T, preferred_element_type=jnp.float32) + jnp.dot(d_up, w_up.T, preferred_element_type=jnp.float32)
        dx = lax.psum(term.astype(jnp.bfloat16), "tp")
        dw_gate = jnp.dot(x.T, d_gate, preferred_element_type=jnp.float32)
        dw_up = jnp.dot(x.T, d_up, preferred_element_type=jnp.float32)
        dw_down = jnp.dot(hidden.astype(jnp.bfloat16).T, dy, preferred_element_type=jnp.float32)
        return dx, *(g.astype(jnp.bfloat16) for g in (dw_gate, dw_up, dw_down))

    tokens, columns, rows = P("dp", None), P(None, "tp"), P("tp", None)
    return jax.shard_map(
        step,
        mesh=mesh,
        in_specs=(tokens, tokens, P("dp", "tp"), P("dp", "tp"), columns, columns, rows),
        out_specs=(tokens, P("dp", "tp"), P("dp", "tp"), P(("dp", "tp"), None)),
        check_vma=False,
    )
```

profile of v0, /device:TPU:0, one launch (start us, length us, event | category | flops | bytes accessed | tf_op | source)
XLA Modules:
  0.0 280.6 jit_solution(3518011862370085629)
XLA Ops:
  7.2 0.0 all-reduce.2.cloned.1.call-start
  7.2 22.6 %fusion.6 = (bf16[2048,640]{1,0:T(8,128)(2,1)}, f32[2048,640]{1,0:T(8,128)}) fusion(bf16[2048,640]{1,0:T(8,128)(2,1)} %param.9, bf16[2048,640]{1,0:T(8,128)(2,1)} %param.10, bf16[2048,4096]{1,0:T(8,128)(2,1)} %param.8, bf16[640,4096]{1,0:T(8,128)(2,1)} %param.13), kind=kOutput, calls=%fused_computation.17 | convolution fusion | flops 10767564800 | bytes 35127296 | tf_op jit(solution)/shard_map/dot_general | solution.py:14
  29.9 0.0 copy-start
  29.9 22.2 %fusion.21 = f32[2048,4096]{1,0:T(8,128)} fusion(bf16[2048,640]{1,0:T(8,128)(2,1)} %get-tuple-element.8, bf16[4096,640]{1,0:T(8,128)(2,1)} %param.11), kind=kOutput, calls=%fused_computation.32 | convolution fusion | flops 10737418240 | bytes 41418752 | tf_op jit(solution)/shard_map/dot_general | solution.py:16
  52.0 0.0 copy-done
  52.0 24.8 %add_convert_fusion = bf16[2048,4096]{1,0:T(8,128)(2,1)} fusion(f32[2048,4096]{1,0:T(8,128)} %fusion.21, bf16[4096,640]{1,0:T(8,128)(2,1)} %param.12, f32[2048,640]{1,0:T(8,128)} %get-tuple-element.9, bf16[2048,640]{1,0:T(8,128)(2,1)S(1)} %copy-done), kind=kOutput, calls=%fused_computation | convolution fusion | flops 10768613376 | bytes 63438848 | tf_op jit(solution)/shard_map/dot_general | solution.py:16
  76.9 0.0 all-reduce.2.cloned.1.call-update
  76.9 17.2 %fusion.1 = bf16[4096,640]{0,1:T(8,128)(2,1)} fusion(bf16[2048,640]{1,0:T(8,128)(2,1)} %get-tuple-element.8, bf16[2048,4096]{1,0:T(8,128)(2,1)} %param.7), kind=kOutput, calls=%fused_computation.12 | convolution fusion | flops 10740039680 | bytes 24641536 | tf_op jit(solution)/shard_map/dot_general | solution.py:18
  94.1 7.8 %copy.11 = bf16[4096,640]{1,0:T(8,128)(2,1)} copy(bf16[4096,640]{0,1:T(8,128)(2,1)} %fusion.1) | data formatting | bytes 10485760
  101.9 20.2 %fusion.2 = bf16[4096,640]{0,1:T(8,128)(2,1)} fusion(bf16[2048,4096]{1,0:T(8,128)(2,1)} %param.7, f32[2048,640]{1,0:T(8,128)} %get-tuple-element.9, bf16[2048,640]{1,0:T(8,128)(2,1)S(1)} %copy-done), kind=kOutput, calls=%fused_computation.13 | convolution fusion | flops 10754457600 | bytes 29884416 | tf_op jit(solution)/shard_map/dot_general | solution.py:19
  122.1 7.8 %copy.12 = bf16[4096,640]{1,0:T(8,128)(2,1)} copy(bf16[4096,640]{0,1:T(8,128)(2,1)} %fusion.2) | data formatting | bytes 10485760
  129.9 19.9 %convolution_convert_fusion = bf16[640,4096]{1,0:T(8,128)(2,1)} fusion(bf16[2048,4096]{1,0:T(8,128)(2,1)} %param.8, bf16[2048,640]{1,0:T(8,128)(2,1)} %param.10, bf16[2048,640]{1,0:T(8,128)(2,1)S(1)} %copy-done), kind=kOutput, calls=%fused_computation.9 | convolution fusion | flops 10755768320 | bytes 27262976 | tf_op jit(solution)/shard_map/dot_general | solution.py:20
  149.8 109.9 %all-reduce.2.cloned.1.call-done = bf16[2048,4096]{1,0:T(8,128)(2,1)} async-done(((bf16[2048,4096]{1,0:T(8,128)(2,1)}), bf16[2048,4096]{1,0:T(8,128)(2,1)}) %all-reduce.2.cloned.1.call-update) | async-done | bytes 16777232 | tf_op jit(solution)/shard_map/psum | solution.py:17
  259.7 14.1 %copy.14 = bf16[2048,4096]{1,0:T(8,128)(2,1)} copy(bf16[2048,4096]{1,0:T(8,128)(2,1)} %all-reduce.2.cloned.1.call-done) | data formatting | bytes 33554432
Async XLA Ops:
  7.2 252.5 %all-reduce.2.cloned.1.call-start = ((), (), s32[]{:S(2)}) async-start(), calls=%async_computation | async-start | bytes 33554432 | tf_op jit(solution)/shard_map/psum | solution.py:17
  29.9 22.2 %copy-start = (bf16[2048,640]{1,0:T(8,128)(2,1)S(1)}, bf16[2048,640]{1,0:T(8,128)(2,1)}, u32[]{:S(2)}) copy-start(bf16[2048,640]{1,0:T(8,128)(2,1)} %param.9) | copy-start | bytes 7864324
Sparse Core Ops, SparseCore 0:
  77.0 182.6 all-reduce.1
where the time goes:
time: 281 us
  matrix products  127 us (45%)
  waiting for transfers between devices  110 us (39%)
  local copies, waits for them, and re-layouts  29.7 us (11%)
  between operations  14 us (5%)
    psum x1, waiting for transfers between devices, step(): dx = lax.psum(term.astype(jnp.bfloat16), 'tp')  110 us
    unnamed x5, local copies, waits for them, and re-layouts  29.7 us
    dot_general x1, matrix products, step(): jnp.dot(d_up, w_up.T, preferred_element_type=jnp.float32)  24.8 us
    dot_general x1, matrix products, step(): d_hidden = jnp.dot(dy, w_down.T, preferred_element_type=jnp.float32)  22.6 us
    dot_general x1, matrix products, step(): jnp.dot(d_gate, w_gate.T, preferred_element_type=jnp.float32)  22.2 us
    dot_general x1, matrix products, step(): dw_up = jnp.dot(x.T, d_up, preferred_element_type=jnp.float32)  20.2 us
    dot_general x1, matrix products, step(): jnp.dot(hidden.astype(jnp.bfloat16).T, dy, preferred_element_type=jnp.flo...  19.9 us
    dot_general x1, matrix products, step(): dw_gate = jnp.dot(x.T, d_gate, preferred_element_type=jnp.float32)  17.2 us
  transfers between devices with their start and end apart: 1, of which 1 were waited for; matrix products, arithmetic and copies ran while one was open for 26% of the time, Pallas kernels for 0%

commit v1 on v0

v1 whole, which is shorter than its diff:
```python
import functools

import jax
import jax.numpy as jnp
from jax import lax
from jax.experimental import pallas as pl
from jax.experimental.pallas import tpu as pltpu
from jax.sharding import PartitionSpec as P

MESH = pl.DeviceIdType.MESH
BF16, F32 = jnp.bfloat16, jnp.float32

ROWS, D, F = 2048, 4096, 640
HALF = ROWS // 2
CW = 256
K = D // CW
BLOCK, SEG = 512, 128

PIECE = (32, 48, 48)
BASE = (0, 512, 1280)
OFF = tuple(tuple(n * o for o in (0, 32, 80)) for n in (8, 4, 2, 1))

LAG_B, LAG_C, LAG_D, LAG_E, LAG_F, LAG_G, LAG_H, LAG_I = 1, 3, 5, 7, 9, 11, 13, 15
STEPS = K + LAG_I
UNIT0 = 8
RING = 8
SENDS = 4


def act(gate, up):
    return jax.nn.gelu(gate) * up


def dot(a, b, ca, cb):
    return lax.dot_general(a, b, (((ca,), (cb,)), ((), ())), preferred_element_type=F32)


def source_row(half, seg):
    return jnp.where(
        seg < 2,
        256 * half + SEG * seg,
        jnp.where(seg < 5, 512 + 384 * half + SEG * (seg - 2), 1280 + 384 * half + SEG * (seg - 5)),
    )


def rows_at(start, n):
    return pl.ds(pl.multiple_of(start, 16), n)


def kernel(
    x, dy, gate, up, w_gate, w_up, w_down, dx, dw_gate, dw_up, dw_down,
    d, ht, w, own, ds, dr, s1, s2, s3, r1, r2, r3, fin,
    w_sem, ds_sem, dr_sem, s_sem, r_sem, fin_sem, as_sem, ar_sem, in_sem, out_sem,
):
    me = lax.axis_index("tp")
    core = me % 2
    bits = ((me // 8) % 2, (me // 4) % 2, (me // 2) % 2)
    step_of = (8, 4, 2)
    partner_core = me + 1 - 2 * core
    partners = tuple(me + s - 2 * s * b for s, b in zip(step_of, bits))

    barrier = pltpu.get_barrier_semaphore()
    for other in (partner_core, *partners):
        pl.semaphore_signal(barrier, inc=1, device_id={"tp": other}, device_id_type=MESH)
    pl.semaphore_wait(barrier, 4)

    def pick(axis, values):
        return jnp.where(axis == 0, values[0], jnp.where(axis == 1, values[1], values[2]))

    def remote(src, dst, send, recv, to):
        return pltpu.make_async_remote_copy(
            src_ref=src, dst_ref=dst, send_sem=send, recv_sem=recv, device_id={"tp": to}, device_id_type=MESH
        )

    def w_copies():
        return (
            pltpu.make_async_copy(w_gate, w.at[:, 0:F], w_sem.at[0]),
            pltpu.make_async_copy(w_up, w.at[:, F : 2 * F], w_sem.at[1]),
        )

    def first(wd, dyb, gb, ub, wd_sem, b_sem):
        def loads(b):
            slot = b % 2
            for s in range(BLOCK // SEG):
                src = pl.ds(pl.multiple_of(source_row(b // 2, (b % 2) * (BLOCK // SEG) + s), SEG), SEG)
                to = pl.ds(s * SEG, SEG)
                yield pltpu.make_async_copy(dy.at[src, :], dyb.at[slot, to, :], b_sem.at[slot, s, 0])
                yield pltpu.make_async_copy(gate.at[src, :], gb.at[slot, to, :], b_sem.at[slot, s, 1])
                yield pltpu.make_async_copy(up.at[src, :], ub.at[slot, to, :], b_sem.at[slot, s, 2])

        wd_copy = pltpu.make_async_copy(w_down, wd, wd_sem)
        wd_copy.start()
        for c in loads(0):
            c.start()

        def body(b, _):
            @pl.when(b + 1 < ROWS // BLOCK)
            def _():
                for c in loads(b + 1):
                    c.start()

            @pl.when(b == 0)
            def _():
                wd_copy.wait()
                for c in w_copies():
                    c.start()

            for c in loads(b):
                c.wait()
            slot = b % 2
            rows = pl.ds(pl.multiple_of(b * BLOCK, BLOCK), BLOCK)
            for lo, hi in ((0, 256), (256, 512), (512, F)):
                d_hidden = dot(dyb[slot], wd[lo:hi, :], 1, 1)
                hidden, back = jax.vjp(act, gb[slot, :, lo:hi].astype(F32), ub[slot, :, lo:hi].astype(F32))
                d_gate, d_up = back(d_hidden)
                d[rows, lo:hi] = d_gate.astype(BF16)
                d[rows, F + lo : F + hi] = d_up.astype(BF16)
                ht[lo:hi, rows] = hidden.T.astype(BF16)
            return 0

        lax.fori_loop(0, ROWS // BLOCK, body, 0)
        for c in w_copies():
            c.wait()

    pl.run_scoped(
        first,
        pltpu.VMEM((F, D), BF16),
        pltpu.VMEM((2, BLOCK, D), BF16),
        pltpu.VMEM((2, BLOCK, F), BF16),
        pltpu.VMEM((2, BLOCK, F), BF16),
        pltpu.SemaphoreType.DMA,
        pltpu.SemaphoreType.DMA((2, BLOCK // SEG, 3)),
    )

    def second(xb, yb, ob, oc):
        def tile_loads(u):
            slot = u % 2
            cols = pl.ds(pl.multiple_of(u * CW, CW), CW)
            for half in range(2):
                for g in range(3):
                    n = 8 * PIECE[g]
                    src = pl.ds(BASE[g] + half * n, n)
                    to = pl.ds(half * HALF + OFF[0][g], n)
                    yield pltpu.make_async_copy(x.at[src, cols], xb.at[slot, to, :], in_sem.at[slot, 0, half, g])
                    yield pltpu.make_async_copy(dy.at[src, cols], yb.at[slot, to, :], in_sem.at[slot, 1, half, g])

        def tile_stores(u):
            slot = u % 2
            at = pl.ds(pl.multiple_of(u * CW, CW), CW)
            yield pltpu.make_async_copy(ob.at[slot, :, 0:F], dw_gate.at[at, :], out_sem.at[slot, 0])
            yield pltpu.make_async_copy(ob.at[slot, :, F : 2 * F], dw_up.at[at, :], out_sem.at[slot, 1])
            yield pltpu.make_async_copy(oc.at[slot], dw_down.at[:, at], out_sem.at[slot, 2])

        def d2d(j):
            return remote(ds.at[j % 2], dr.at[j % SENDS], ds_sem.at[j % 2], dr_sem.at[j % SENDS], partner_core)

        sent, got = (s1, s2, s3), (r1, r2, r3)

        def scatter(stage, g, j):
            n = PIECE[g] * (4, 2, 1)[stage]
            at = pl.ds(OFF[stage + 1][g], n)
            return remote(
                sent[stage].at[j % SENDS, at, :],
                got[stage].at[j, at, :],
                s_sem.at[stage, g, j % SENDS],
                r_sem.at[stage, g, j],
                pick((g + j + stage) % 3, partners),
            )

        def place(g, j, stage, theirs):
            p = PIECE[g]
            ba, bb, bc = (pick((g + j + s) % 3, bits) for s in range(3))
            if stage == 0:
                at = 8 * core + 4 * ba + 2 * bb + (1 - bc if theirs else bc)
            elif stage == 1:
                at = 8 * core + 4 * ba + 2 * (1 - bb if theirs else bb)
            elif stage == 2:
                at = 8 * core + 4 * (1 - ba if theirs else ba)
            else:
                at = 8 * (1 - core if theirs else core)
            n = p * (1, 2, 4, 8)[stage]
            return dx.at[rows_at(BASE[g] + p * at, n), pl.ds(pl.multiple_of(j * CW, CW), CW)]

        def fin_at(g, j):
            return fin.at[j % SENDS, pl.ds(OFF[3][g], PIECE[g]), :]

        def fin_copy(g, j):
            return pltpu.make_async_copy(fin_at(g, j), place(g, j, 0, False), fin_sem.at[g, j % SENDS])

        def gather(stage, g, j, theirs):
            spot = place(g, j, stage, theirs)
            to = partner_core if stage == 3 else pick((g + j + 2 - stage) % 3, partners)
            src = fin_at(g, j) if stage == 0 else spot
            return remote(src, spot, as_sem.at[stage, g, j % SENDS], ar_sem.at[stage, g, j], to)

        def when_chunk(i, lag):
            j = i - lag
            return j, pl.when(jnp.logical_and(j >= 0, j < K))

        def body(i, _):
            @pl.when(i < K)
            def _():
                wt = pl.ds(pl.multiple_of(i * CW, CW), CW)

                @pl.when(i >= 2)
                def _():
                    d2d(i - 2).wait_send()

                def part(half, r):
                    rows = pl.ds(pl.multiple_of(half * HALF + r * BLOCK, BLOCK), BLOCK)
                    return dot(d[rows, :], w[wt, :], 1, 1), pl.ds(pl.multiple_of(r * BLOCK, BLOCK), BLOCK)

                @pl.loop(0, HALF // BLOCK)
                def _(r):
                    term, at = part(1 - core, r)
                    ds[i % 2, at, :] = term.astype(BF16)

                d2d(i).start()

                @pl.loop(0, HALF // BLOCK)
                def _(r):
                    term, at = part(core, r)
                    own[i % RING, at, :] = term

            j, valid = when_chunk(i, LAG_B)

            @valid
            def _():
                d2d(j).wait_recv()
                for g in range(3):
                    n = 4 * PIECE[g]
                    bit = pick((g + j) % 3, bits)
                    keep = rows_at(OFF[0][g] + n * bit, n)
                    give = rows_at(OFF[0][g] + n * (1 - bit), n)
                    at = pl.ds(OFF[1][g], n)

                    @pl.when(j >= SENDS)
                    def _():
                        scatter(0, g, j - SENDS).wait_send()

                    s1[j % SENDS, at, :] = (own[j % RING, give, :] + dr[j % SENDS, give, :].astype(F32)).astype(BF16)
                    scatter(0, g, j).start()
                    own[j % RING, keep, :] = own[j % RING, keep, :] + dr[j % SENDS, keep, :].astype(F32)

            for stage, lag in ((1, LAG_C), (2, LAG_D)):
                j, valid = when_chunk(i, lag)

                @valid
                def _(j=j, stage=stage):
                    for g in range(3):
                        scatter(stage - 1, g, j).wait_recv()
                        n = PIECE[g] * (4, 2, 1)[stage]
                        bs = [pick((g + j + s) % 3, bits) for s in range(stage + 1)]
                        start = OFF[0][g] + sum(PIECE[g] * (4, 2, 1)[s] * bs[s] for s in range(stage))
                        bit = bs[stage]
                        keep, give = rows_at(start + n * bit, n), rows_at(start + n * (1 - bit), n)
                        base = OFF[stage][g]
                        rkeep, rgive = rows_at(base + n * bit, n), rows_at(base + n * (1 - bit), n)
                        at = pl.ds(OFF[stage + 1][g], n)

                        @pl.when(j >= SENDS)
                        def _():
                            scatter(stage, g, j - SENDS).wait_send()

                        r = got[stage - 1]
                        sent[stage][j % SENDS, at, :] = (
                            own[j % RING, give, :] + r[j, rgive, :].astype(F32)
                        ).astype(BF16)
                        scatter(stage, g, j).start()
                        own[j % RING, keep, :] = own[j % RING, keep, :] + r[j, rkeep, :].astype(F32)

            j, valid = when_chunk(i, LAG_E)

            @valid
            def _():
                for g in range(3):
                    scatter(2, g, j).wait_recv()
                    n = PIECE[g]
                    bs = [pick((g + j + s) % 3, bits) for s in range(3)]
                    keep = rows_at(OFF[0][g] + sum(n * (4, 2, 1)[s] * bs[s] for s in range(3)), n)
                    at = pl.ds(OFF[3][g], n)

                    @pl.when(j >= SENDS)
                    def _():
                        gather(0, g, j - SENDS, False).wait_send()

                    fin[j % SENDS, at, :] = (own[j % RING, keep, :] + r3[j, at, :].astype(F32)).astype(BF16)
                    fin_copy(g, j).start()
                    gather(0, g, j, False).start()

            for stage, lag in ((1, LAG_F), (2, LAG_G), (3, LAG_H)):
                j, valid = when_chunk(i, lag)

                @valid
                def _(j=j, stage=stage):
                    for g in range(3):
                        gather(stage - 1, g, j, True).wait_recv()
                        if stage == 1:
                            fin_copy(g, j).wait()

                        @pl.when(j >= SENDS)
                        def _():
                            gather(stage, g, j - SENDS, False).wait_send()

                        gather(stage, g, j, False).start()

            j, valid = when_chunk(i, LAG_I)

            @valid
            def _():
                for g in range(3):
                    gather(3, g, j, True).wait_recv()

            u = i - UNIT0

            @pl.when(u == -1)
            def _():
                for c in tile_loads(0):
                    c.start()

            @pl.when(jnp.logical_and(u >= 0, u < K))
            def _():
                @pl.when(u + 1 < K)
                def _():
                    for c in tile_loads(u + 1):
                        c.start()

                for c in tile_loads(u):
                    c.wait()

                @pl.when(u >= 2)
                def _():
                    for c in tile_stores(u - 2):
                        c.wait()

                slot = u % 2
                ob[slot] = dot(xb[slot], d[...], 0, 0).astype(BF16)
                oc[slot] = dot(ht[...], yb[slot], 1, 0).astype(BF16)
                for c in tile_stores(u):
                    c.start()

            return 0

        lax.fori_loop(0, STEPS, body, 0)

        for u in (K - 2, K - 1):
            for c in tile_stores(u):
                c.wait()
        for j in (K - 2, K - 1):
            d2d(j).wait_send()
        for j in range(K - SENDS, K):
            for g in range(3):
                for stage in range(3):
                    scatter(stage, g, j).wait_send()
                for stage in range(4):
                    gather(stage, g, j, False).wait_send()

    pl.run_scoped(
        second,
        pltpu.VMEM((2, ROWS, CW), BF16),
        pltpu.VMEM((2, ROWS, CW), BF16),
        pltpu.VMEM((2, CW, 2 * F), BF16),
        pltpu.VMEM((2, F, CW), BF16),
    )


def solution(mesh):
    def step(x, dy, gate, up, w_gate, w_up, w_down):
        shape = lambda *s: jax.ShapeDtypeStruct(s, BF16)
        anywhere = pl.BlockSpec(memory_space=pl.ANY)
        dma = pltpu.SemaphoreType.DMA
        return pl.pallas_call(
            kernel,
            out_shape=(shape(ROWS, D), shape(D, F), shape(D, F), shape(F, D)),
            in_specs=[anywhere] * 7,
            out_specs=(anywhere,) * 4,
            scratch_shapes=[
                pltpu.VMEM((ROWS, 2 * F), BF16),
                pltpu.VMEM((F, ROWS), BF16),
                pltpu.VMEM((D, 2 * F), BF16),
                pltpu.VMEM((RING, HALF, CW), F32),
                pltpu.VMEM((2, HALF, CW), BF16),
                pltpu.VMEM((SENDS, HALF, CW), BF16),
                pltpu.VMEM((SENDS, 512, CW), BF16),
                pltpu.VMEM((SENDS, 256, CW), BF16),
                pltpu.VMEM((SENDS, 128, CW), BF16),
                pltpu.VMEM((K, 512, CW), BF16),
                pltpu.VMEM((K, 256, CW), BF16),
                pltpu.VMEM((K, 128, CW), BF16),
                pltpu.VMEM((SENDS, 128, CW), BF16),
                dma((2,)),
                dma((2,)),
                dma((SENDS,)),
                dma((3, 3, SENDS)),
                dma((3, 3, K)),
                dma((3, SENDS)),
                dma((4, 3, SENDS)),
                dma((4, 3, K)),
                dma((2, 2, 2, 3)),
                dma((2, 3)),
            ],
            compiler_params=pltpu.CompilerParams(
                collective_id=0, has_side_effects=True, vmem_limit_bytes=67043328
            ),
        )(x, dy, gate, up, w_gate, w_up, w_down)

    tokens, columns, rows = P("dp", None), P(None, "tp"), P("tp", None)
    return jax.shard_map(
        step,
        mesh=mesh,
        in_specs=(tokens, tokens, P("dp", "tp"), P("dp", "tp"), columns, columns, rows),
        out_specs=(tokens, P("dp", "tp"), P("dp", "tp"), P(("dp", "tp"), None)),
        check_vma=False,
    )
```

time: 281 us -> 168 us (0.60)
  Pallas kernels: 0 us -> 143 us
  matrix products: 127 us -> 0 us
  waiting for transfers between devices: 110 us -> 0 us
  between operations: 14 us -> 0.66 us
  local copies, waits for them, and re-layouts: 29.7 us -> 24.2 us
    pallas_call x0 -> x1, Pallas kernels: none -> 143 us  [step(): pl.pallas_call(kernel, out_shape=(shape(ROWS, D), shape(D, F), shape(D, F...]
    dot_general x6 -> x0, matrix products: 127 us -> none  [the longest x1 24.8 us: step(): jnp.dot(d_up, w_up.T, preferred_element_type=jnp.float32)]
    psum x1 -> x0, waiting for transfers between devices: 110 us -> none  [step(): dx = lax.psum(term.astype(jnp.bfloat16), 'tp')]
    unnamed x5 -> x12, local copies, waits for them, and re-layouts: 29.7 us -> 24.2 us
  transfers between devices with their start and end apart: 1 -> 0, of which waited for: 1 -> 0; matrix products, arithmetic and copies ran while one was open for 26% -> 0% of each run, Pallas kernels for 0% -> 0%
where the time goes in v1:
time: 168 us
  Pallas kernels  143 us (85%)
  local copies, waits for them, and re-layouts  24.2 us (14%)
    pallas_call x1, Pallas kernels, step(): pl.pallas_call(kernel, out_shape=(shape(ROWS, D), shape(D, F), shape(D, F...  143 us
    unnamed x12, local copies, waits for them, and re-layouts  24.2 us

profile of v1, /device:TPU:0, one launch (start us, length us, event | category | flops | bytes accessed | tf_op | source)
XLA Modules:
  0.0 168.3 jit_solution(18064433679741450410)
XLA Ops:
  0.6 143.5 %shard_map.102 = (bf16[2048,4096]{1,0:T(8,128)(2,1)}, bf16[4096,640]{1,0:T(8,128)(2,1)}, bf16[4096,640]{1,0:T(8,128)(2,1)}, bf16[640,4096]{1,0:T(8,128)(2,1)}) custom-call(bf16[2048,4096]{1,0:T(8,128)(2,1)} %x.1, bf16[2048,4096]{1,0:T(8,128)(2,1)} %dy.1, bf16[2048,640]{1,0:T(8,128)(2,1)} %gate.1, bf16[2048,640]{1,0:T(8,128)(2,1)} %up.1, ...), custom_call_target="tpu_custom_call" | custom-call | tf_op jit(solution)/shard_map/pallas_call | solution.py:372
  144.1 0.0 copy-start.1
  144.1 14.4 %copy.15 = bf16[2048,4096]{1,0:T(8,128)(2,1)} copy(bf16[2048,4096]{1,0:T(8,128)(2,1)} %get-tuple-element.8) | data formatting | bytes 33554432
  158.5 0.0 copy-done.1
  158.5 0.0 copy-start
  158.5 0.0 slice-start
  158.5 2.7 %copy.16 = bf16[4096,640]{1,0:T(8,128)(2,1)} copy(bf16[4096,640]{1,0:T(8,128)(2,1)S(1)} %copy-done.1) | data formatting | bytes 10485760
  161.2 1.7 %copy-done = bf16[4096,640]{1,0:T(8,128)(2,1)S(1)} copy-done((bf16[4096,640]{1,0:T(8,128)(2,1)S(1)}, bf16[4096,640]{1,0:T(8,128)(2,1)}, u32[]{:S(2)}) %copy-start) | copy-done | bytes 5242904
  162.9 0.0 slice-start.1
  162.9 2.4 %copy.17 = bf16[4096,640]{1,0:T(8,128)(2,1)} copy(bf16[4096,640]{1,0:T(8,128)(2,1)S(1)} %copy-done) | data formatting | bytes 10485760
  165.3 0.0 slice-done
  165.3 0.6 slice-done.1
  166.0 2.4 %copy.18 = bf16[640,4096]{1,0:T(8,128)(2,1)} copy(bf16[640,4096]{1,0:T(8,128)(2,1)S(1)} %bitcast.1) | data formatting | bytes 10485760
  (1 shorter events, 0.0 us)
Async XLA Ops:
  144.1 14.4 %copy-start.1 = (bf16[4096,640]{1,0:T(8,128)(2,1)S(1)}, bf16[4096,640]{1,0:T(8,128)(2,1)}, u32[]{:S(2)}) copy-start(bf16[4096,640]{1,0:T(8,128)(2,1)} %get-tuple-element.9) | copy-start | bytes 15728644
  158.5 4.4 %copy-start = (bf16[4096,640]{1,0:T(8,128)(2,1)S(1)}, bf16[4096,640]{1,0:T(8,128)(2,1)}, u32[]{:S(2)}) copy-start(bf16[4096,640]{1,0:T(8,128)(2,1)} %get-tuple-element.10) | copy-start | bytes 15728644
  158.5 6.8 %slice-start = ((s8[5242880]{0:T(1024)(128)(4,1)}), s8[4194304]{0:T(1024)(128)(4,1)S(1)}, s32[]{:S(2)}) async-start(s8[5242880]{0:T(1024)(128)(4,1)} %bitcast), calls=%async_computation | async-start | bytes 8388608
  162.9 3.1 %slice-start.1 = ((s8[5242880]{0:T(1024)(128)(4,1)}), s8[1048576]{0:T(1024)(128)(4,1)S(1)}, s32[]{:S(2)}) async-start(s8[5242880]{0:T(1024)(128)(4,1)} %bitcast), calls=%async_computation.1 | async-start | bytes 2097152
